TPU v7x, 32 devices: a whole 2x2x4 slice. The times are simulated.
32 devices in a mesh: dp: 8 (over z, x), txt: 4 (over y, core).
Axes of the slice: x: 2, y: 2, z: 4, core: 2. Of those that a mesh axis runs over, the one named last changes fastest.
Arguments:
- resid: bfloat16 [2048, 1024], P('dp', 'txt'), may hold values from -40 to 40
- prenorm_gain: float32 [1024], replicated, may hold values from 0.25 to 1.75
- prenorm_bias: float32 [1024], replicated, may hold values from -3 to 3
- up_weight: bfloat16 [1024, 4096], P('dp', 'txt'), may hold values from -0.1875 to 0.1875
- up_bias: float32 [4096], P('txt'), may hold values from -3 to 3
- down_weight: bfloat16 [4096, 1024], P('txt', 'dp'), may hold values from -0.09375 to 0.09375
- down_bias: float32 [1024], replicated, may hold values from -3 to 3
- post_gain: float32 [1024], P('txt'), may hold values from 0.25 to 1.75
- post_bias: float32 [1024], P('txt'), may hold values from -3 to 3
- projection: bfloat16 [1024, 768], P('txt'), may hold values from -1 to 1
- texts: bfloat16 [5120, 768], P('txt'), may hold values from -48 to 48
- labels: int32 [2048], P('dp'), may hold values from 0 to 5119
- step_size: float32 [1], replicated, may hold values from 0.5 to 2
Outputs:
- adversarial: float32 [2048, 1024], P('dp', 'txt')
All inputs are finite; a program needn't handle non-finite values.
Results may differ from a plain program's by a relative error of at most 0.0036.
Values may be sent and summed in bfloat16 or wider, within the bound.
A program may use at most 64 MiB of HBM per device.

v0:
```python
import jax
import jax.numpy as jnp
from jax import lax
from jax.sharding import PartitionSpec as P

MODEL_WIDTH = 1024


def local(
    resid,
    prenorm_gain,
    prenorm_bias,
    up_weight,
    up_bias,
    down_weight,
    down_bias,
    post_gain,
    post_bias,
    projection,
    texts,
    labels,
    step_size,
):
    feature_width = resid.shape[1]
    shift_amount = lax.axis_index("txt") * feature_width
    gathered = lax.all_gather(resid, "txt", axis=1, tiled=True)
    input_rows = gathered.astype(jnp.float32)
    input_mean = jnp.mean(input_rows, axis=1, keepdims=True)
    var_in = jnp.mean(input_rows * input_rows, axis=1, keepdims=True) - input_mean * input_mean
    input_inverse_deviation = lax.rsqrt(var_in + 1e-05)
    centered_input = (input_rows - input_mean) * input_inverse_deviation
    normed_input = (centered_input * prenorm_gain + prenorm_bias).astype(jnp.bfloat16)
    w_up = lax.all_gather(up_weight, "dp", axis=0, tiled=True)
    w_down = lax.all_gather(down_weight, "dp", axis=1, tiled=True)
    pre_act = jnp.dot(normed_input, w_up, preferred_element_type=jnp.float32) + up_bias
    gate_sig = jax.nn.sigmoid(1.702 * pre_act)
    hidden = (pre_act * gate_sig).astype(jnp.bfloat16)
    mixed_part = jnp.dot(hidden, w_down, preferred_element_type=jnp.float32)
    mixed = lax.psum_scatter(mixed_part, "txt", scatter_dimension=1, tiled=True)
    own_rows = resid.astype(jnp.float32)
    block_out = own_rows + mixed + lax.dynamic_slice_in_dim(down_bias, shift_amount, feature_width)
    out_sums = lax.psum((jnp.sum(block_out, axis=1), jnp.sum(block_out * block_out, axis=1)), "txt")
    mean_out = out_sums[0][:, None] / MODEL_WIDTH
    var_out = out_sums[1][:, None] / MODEL_WIDTH - mean_out * mean_out
    rstd_out = lax.rsqrt(var_out + 1e-05)
    yhat = (block_out - mean_out) * rstd_out
    post_normed = (yhat * post_gain + post_bias).astype(jnp.bfloat16)
    emb_part = jnp.dot(post_normed, projection, preferred_element_type=jnp.float32)
    embedding = lax.psum_scatter(emb_part, "txt", scatter_dimension=0, tiled=True)
    emb_norm = jnp.sqrt(jnp.sum(embedding * embedding, axis=1, keepdims=True) + 1e-06)
    unit_vec = embedding / emb_norm
    unit_low = lax.all_gather(unit_vec.astype(jnp.bfloat16), "txt", axis=0, tiled=True)
    text_f = texts.astype(jnp.float32)
    text_unit = (text_f / jnp.sqrt(jnp.sum(text_f * text_f, axis=1, keepdims=True) + 1e-06)).astype(
        jnp.bfloat16
    )
    logits = 100.0 * jnp.einsum(
        "ie,je->ij", unit_low, text_unit, preferred_element_type=jnp.float32
    )
    local_top = jnp.max(logits, axis=1)
    row_top = lax.pmax(local_top, "txt")
    exponent = jnp.exp(logits - row_top[:, None])
    row_total = lax.psum(jnp.sum(exponent, axis=1), "txt")
    prob = exponent / row_total[:, None]
    local_label = labels - lax.axis_index("txt") * texts.shape[0]
    columns = lax.broadcasted_iota(jnp.int32, logits.shape, 1)
    target = (columns == local_label[:, None]).astype(jnp.float32)
    score_grad = (100.0 * (prob - target)).astype(jnp.bfloat16)
    back_part = jnp.dot(score_grad, text_unit, preferred_element_type=jnp.float32)
    unit_grad = lax.psum_scatter(back_part, "txt", scatter_dimension=0, tiled=True)
    along = jnp.sum(unit_vec * unit_grad, axis=1, keepdims=True)
    grad_share = ((unit_grad - unit_vec * along) / emb_norm).astype(jnp.bfloat16)
    emb_grad = lax.all_gather(grad_share, "txt", axis=0, tiled=True)
    post_grad = jnp.einsum("ie,de->id", emb_grad, projection, preferred_element_type=jnp.float32)
    scaled = post_grad * post_gain
    back_sums = lax.psum((jnp.sum(scaled, axis=1), jnp.sum(scaled * yhat, axis=1)), "txt")
    output_gradient = (
        scaled - back_sums[0][:, None] / MODEL_WIDTH - yhat * (back_sums[1][:, None] / MODEL_WIDTH)
    ) * rstd_out
    out_full = lax.all_gather(output_gradient.astype(jnp.bfloat16), "txt", axis=1, tiled=True)
    hid_grad = jnp.einsum("id,fd->if", out_full, w_down, preferred_element_type=jnp.float32)
    act_grad = (hid_grad * (gate_sig + 1.702 * pre_act * gate_sig * (1.0 - gate_sig))).astype(
        jnp.bfloat16
    )
    normed_part = jnp.einsum("if,df->id", act_grad, w_up, preferred_element_type=jnp.float32)
    normed_gradient = lax.psum_scatter(normed_part, "txt", scatter_dimension=1, tiled=True)
    centered_input_portion = lax.dynamic_slice_in_dim(
        centered_input, shift_amount, feature_width, 1
    )
    scaled_input = normed_gradient * lax.dynamic_slice_in_dim(
        prenorm_gain, shift_amount, feature_width
    )
    input_row_sums = lax.psum(
        (jnp.sum(scaled_input, axis=1), jnp.sum(scaled_input * centered_input_portion, axis=1)),
        "txt",
    )
    input_gradient = (
        output_gradient
        + (
            scaled_input
            - input_row_sums[0][:, None] / MODEL_WIDTH
            - centered_input_portion * (input_row_sums[1][:, None] / MODEL_WIDTH)
        )
        * input_inverse_deviation
    )
    square_sum = lax.psum(jnp.sum(input_gradient * input_gradient, axis=1), "txt")
    grad_rms = jnp.sqrt(square_sum[:, None] / MODEL_WIDTH + 1e-06)
    return own_rows + step_size[0] * input_gradient / grad_rms


def solution(mesh):
    placed = (
        P("dp", "txt"),
        P(),
        P(),
        P("dp", "txt"),
        P("txt"),
        P("txt", "dp"),
        P(),
        P("txt"),
        P("txt"),
        P("txt", None),
        P("txt", None),
        P("dp"),
        P(),
    )
    return jax.shard_map(
        local, mesh=mesh, in_specs=placed, out_specs=P("dp", "txt"), check_vma=False
    )
```

profile of v0, /device:TPU:0, one launch (start us, length us, event | category | flops | bytes accessed | tf_op | source)
XLA Modules:
  0.0 297.3 jit_solution(12234471146780298693)
XLA Ops:
  8.1 8.9 %all_gather.18 = bf16[256,1024]{1,0:T(8,128)(2,1)S(1)} all-gather(bf16[256,256]{1,0:T(8,128)(2,1)} %param.13), channel_id=1, replica_groups=mesh['dp'=8,'txt'=4] {'txt'}, dimensions={1}, use_global_device_ids=true | all-gather | bytes 655360 | tf_op jit(solution)/shard_map/all_gather | solution.py:26
  17.2 44.1 %all-gather.3.cloned.1.call-done = bf16[1024,1024]{1,0:T(8,128)(2,1)} async-done(((bf16[128,1024]{1,0:T(8,128)(2,1)}), bf16[1024,1024]{1,0:T(8,128)(2,1)}) %all-gather.3.cloned.1.call-update) | async-done | bytes 2097168 | tf_op jit(solution)/shard_map/all_gather | solution.py:33
  61.3 2.4 convolution_add_fusion
  63.7 48.5 %all-gather.5.cloned.1.call-done = bf16[1024,1024]{1,0:T(8,128)(2,1)} async-done(((bf16[1024,128]{1,0:T(8,128)(2,1)}), bf16[1024,1024]{1,0:T(8,128)(2,1)}) %all-gather.5.cloned.1.call-update) | async-done | bytes 2097168 | tf_op jit(solution)/shard_map/all_gather | solution.py:34
  112.3 3.3 %fusion.17 = f32[256,1024]{1,0:T(8,128)} fusion(bf16[1024,1024]{1,0:T(8,128)(2,1)} %all-gather.5.cloned.1.call-done, f32[256,1024]{1,0:T(8,128)S(1)} %convolution_add_fusion), kind=kOutput, calls=%fused_computation.32 | convolution fusion | flops 538443776 | bytes 4194304 | tf_op jit(solution)/shard_map/dot_general | solution.py:38
  116.6 22.2 %reduce-scatter.5.cloned.1.call-done = f32[256,256]{1,0:T(8,128)} async-done(((f32[256,1024]{1,0:T(8,128)}), f32[256,256]{1,0:T(8,128)}) %reduce-scatter.5.cloned.1.call-update) | async-done | bytes 262160 | tf_op jit(solution)/shard_map/reduce_scatter | solution.py:39
  139.8 5.8 %all-reduce.2 = (f32[256]{0:T(256)S(1)}, f32[256]{0:T(256)S(1)}) all-reduce(f32[256]{0:T(256)S(1)} %get-tuple-element.12, f32[256]{0:T(256)S(1)} %get-tuple-element.11), channel_id=1, replica_groups=mesh['dp'=8,'txt'=4] {'txt'}, use_global_device_ids=true, to_apply=%region_6.0 | all-reduce | flops 512 | bytes 4096 | tf_op jit(solution)/shard_map/psum | solution.py:42
  145.6 1.2 fusion.25
  147.4 1.7 fusion.1
  149.2 21.7 %reduce-scatter.7.cloned.1.call-done = f32[64,768]{1,0:T(8,128)} async-done(((f32[256,768]{1,0:T(8,128)}), f32[64,768]{1,0:T(8,128)}) %reduce-scatter.7.cloned.1.call-update) | async-done | bytes 196624 | tf_op jit(solution)/shard_map/reduce_scatter | solution.py:49
  173.0 6.1 %all_gather.21 = bf16[256,768]{1,0:T(8,128)(2,1)S(1)} all-gather(bf16[64,768]{1,0:T(8,128)(2,1)S(1)} %fusion.35), channel_id=1, replica_groups=mesh['dp'=8,'txt'=4] {'txt'}, dimensions={0}, use_global_device_ids=true | all-gather | bytes 491520 | tf_op jit(solution)/shard_map/all_gather | solution.py:52
  179.1 3.5 %fusion.41 = (f32[256]{0:T(256)S(1)}, f32[256,1280]{1,0:T(8,128)}) fusion(bf16[256,768]{1,0:T(8,128)(2,1)S(1)} %all_gather.21, bf16[1280,768]{1,0:T(8,128)(2,1)} %fusion.1), kind=kOutput, calls=%fused_computation.81 | convolution fusion | flops 503971584 | bytes 3671040 | tf_op jit(solution)/shard_map/ie,je->ij/dot_general | solution.py:57
  182.6 6.4 %pmax.7 = f32[256]{0:T(256)S(1)} all-reduce(f32[256]{0:T(256)S(1)} %get-tuple-element.28), channel_id=1, replica_groups=mesh['dp'=8,'txt'=4] {'txt'}, use_global_device_ids=true, to_apply=%region_11.0 | all-reduce | flops 256 | bytes 2048 | tf_op jit(solution)/shard_map/pmax | solution.py:61
  189.0 1.6 fusion.3
  190.7 5.7 %psum.58 = f32[256]{0:T(256)S(1)} all-reduce(f32[256]{0:T(256)S(1)} %fusion.3), channel_id=1, replica_groups=mesh['dp'=8,'txt'=4] {'txt'}, use_global_device_ids=true, to_apply=%region_13.0 | all-reduce | flops 256 | bytes 2048 | tf_op jit(solution)/shard_map/psum | solution.py:63
  196.3 3.2 %fusion.12 = f32[256,768]{1,0:T(8,128)} fusion(bf16[1280,768]{1,0:T(8,128)(2,1)S(1)} %copy-done.2, f32[256,1280]{1,0:T(8,128)} %get-tuple-element.29, s32[256]{0:T(256)S(1)} %broadcast_subtract_fusion, f32[256]{0:T(256)S(1)} %psum.58, f32[256]{0:T(256)S(1)} %pmax.7), kind=kOutput, calls=%fused_computation.27 | convolution fusion | flops 505610240 | bytes 4066304 | tf_op jit(solution)/shard_map/dot_general | solution.py:69
  199.6 23.9 %reduce-scatter.9.cloned.1.call-done = f32[64,768]{1,0:T(8,128)} async-done(((f32[256,768]{1,0:T(8,128)}), f32[64,768]{1,0:T(8,128)}) %reduce-scatter.9.cloned.1.call-update) | async-done | bytes 196624 | tf_op jit(solution)/shard_map/reduce_scatter | solution.py:70
  225.8 6.1 %all_gather.22 = bf16[256,768]{1,0:T(8,128)(2,1)S(1)} all-gather(bf16[64,768]{1,0:T(8,128)(2,1)S(1)} %divide_convert_fusion), channel_id=1, replica_groups=mesh['dp'=8,'txt'=4] {'txt'}, dimensions={0}, use_global_device_ids=true | all-gather | bytes 491520 | tf_op jit(solution)/shard_map/all_gather | solution.py:73
  232.3 6.5 %all-reduce.1 = (f32[256]{0:T(256)S(1)}, f32[256]{0:T(256)S(1)}) all-reduce(f32[256]{0:T(256)S(1)} %get-tuple-element.10, f32[256]{0:T(256)S(1)} %get-tuple-element.9), channel_id=1, replica_groups=mesh['dp'=8,'txt'=4] {'txt'}, use_global_device_ids=true, to_apply=%region_19.0 | all-reduce | flops 512 | bytes 4096 | tf_op jit(solution)/shard_map/psum | solution.py:76
  239.0 6.9 %all_gather.23 = bf16[256,1024]{1,0:T(8,128)(2,1)S(1)} all-gather(bf16[256,256]{1,0:T(8,128)(2,1)S(1)} %get-tuple-element.21), channel_id=1, replica_groups=mesh['dp'=8,'txt'=4] {'txt'}, dimensions={1}, use_global_device_ids=true | all-gather | bytes 655360 | tf_op jit(solution)/shard_map/all_gather | solution.py:80
  245.9 4.7 %fusion.4 = f32[256,1024]{1,0:T(8,128)} fusion(bf16[1024,1024]{1,0:T(8,128)(2,1)} %all-gather.3.cloned.1.call-done, bf16[256,1024]{1,0:T(8,128)(2,1)S(1)} %all_gather.23, bf16[1024,1024]{1,0:T(8,128)(2,1)} %all-gather.5.cloned.1.call-done, f32[256,1024]{1,0:T(8,128)S(1)} %copy-done.9), kind=kOutput, calls=%fused_computation.16 | convolution fusion | flops 1076363264 | bytes 6815744 | tf_op jit(solution)/shard_map/if,df->id/dot_general | solution.py:85
  252.3 23.6 %reduce-scatter.11.cloned.1.call-done = f32[256,256]{1,0:T(8,128)} async-done(((f32[256,1024]{1,0:T(8,128)}), f32[256,256]{1,0:T(8,128)}) %reduce-scatter.11.cloned.1.call-update) | async-done | bytes 262160 | tf_op jit(solution)/shard_map/reduce_scatter | solution.py:86
  276.9 5.8 %all-reduce = (f32[256]{0:T(256)S(1)}, f32[256]{0:T(256)S(1)}) all-reduce(f32[256]{0:T(256)S(1)} %get-tuple-element.8, f32[256]{0:T(256)S(1)} %get-tuple-element.7), channel_id=1, replica_groups=mesh['dp'=8,'txt'=4] {'txt'}, use_global_device_ids=true, to_apply=%region_24.0 | all-reduce | flops 512 | bytes 4096 | tf_op jit(solution)/shard_map/psum | solution.py:93
  283.9 5.7 %psum.63 = f32[256]{0:T(256)S(1)} all-reduce(f32[256]{0:T(256)S(1)} %get-tuple-element.19), channel_id=1, replica_groups=mesh['dp'=8,'txt'=4] {'txt'}, use_global_device_ids=true, to_apply=%region_26.0 | all-reduce | flops 256 | bytes 2048 | tf_op jit(solution)/shard_map/psum | solution.py:106
  (56 shorter events, 13.5 us)
Async XLA Ops:
  6.5 139.1 %copy-start = (bf16[256,768]{1,0:T(8,128)(2,1)S(1)}, bf16[256,768]{1,0:T(8,128)(2,1)}, u32[]{:S(2)}) copy-start(bf16[256,768]{1,0:T(8,128)(2,1)} %param.22) | copy-start | bytes 1179652
  6.5 54.8 %all-gather.3.cloned.1.call-start = ((), (), s32[]{:S(2)}) async-start(), calls=%async_computation.4 | async-start | bytes 2359296 | tf_op jit(solution)/shard_map/all_gather | solution.py:33
  7.3 105.0 %all-gather.5.cloned.1.call-start = ((), (), s32[]{:S(2)}) async-start(), calls=%async_computation.5 | async-start | bytes 2359296 | tf_op jit(solution)/shard_map/all_gather | solution.py:34
  8.0 130.7 %reduce-scatter.5.cloned.1.call-start = ((), (), s32[]{:S(2)}) async-start(), calls=%async_computation.6 | async-start | bytes 1310720 | tf_op jit(solution)/shard_map/reduce_scatter | solution.py:39
  63.7 51.9 %copy-start.8 = (f32[256,1024]{1,0:T(8,128)}, f32[256,1024]{1,0:T(8,128)S(1)}, u32[]{:S(2)}) copy-start(f32[256,1024]{1,0:T(8,128)S(1)} %convolution_add_fusion) | copy-start | bytes 3145732
  63.7 75.0 %copy-start.4 = (bf16[256,256]{1,0:T(8,128)(2,1)S(1)}, bf16[256,256]{1,0:T(8,128)(2,1)}, u32[]{:S(2)}) copy-start(bf16[256,256]{1,0:T(8,128)(2,1)} %param.13) | copy-start | bytes 393220
  63.7 81.9 %copy-start.5 = (f32[256]{0:T(256)S(1)}, f32[256]{0:T(256)}, u32[]{:S(2)}) copy-start(f32[256]{0:T(256)} %param.20) | copy-start | bytes 3076
  63.7 81.9 %copy-start.7 = (f32[256]{0:T(256)S(1)}, f32[256]{0:T(256)}, u32[]{:S(2)}) copy-start(f32[256]{0:T(256)} %param.21) | copy-start | bytes 3076
  115.6 31.4 %copy-start.6 = (s32[256]{0:T(256)S(1)}, s32[256]{0:T(256)}, u32[]{:S(2)}) copy-start(s32[256]{0:T(256)} %param.24) | copy-start | bytes 3076
  115.6 31.4 %copy-start.1 = (bf16[1280,768]{1,0:T(8,128)(2,1)S(1)}, bf16[1280,768]{1,0:T(8,128)(2,1)}, u32[]{:S(2)}) copy-start(bf16[1280,768]{1,0:T(8,128)(2,1)} %param.23) | copy-start | bytes 5898244
  115.6 55.3 %reduce-scatter.7.cloned.1.call-start = ((), (), s32[]{:S(2)}) async-start(), calls=%async_computation.7 | async-start | bytes 983040 | tf_op jit(solution)/shard_map/reduce_scatter | solution.py:49
  146.9 76.6 %reduce-scatter.9.cloned.1.call-start = ((), (), s32[]{:S(2)}) async-start(), calls=%async_computation.8 | async-start | bytes 983040 | tf_op jit(solution)/shard_map/reduce_scatter | solution.py:70
  179.1 17.2 %copy-start.2 = (bf16[1280,768]{1,0:T(8,128)(2,1)S(1)}, bf16[1280,768]{1,0:T(8,128)(2,1)}, u32[]{:S(2)}) copy-start(bf16[1280,768]{1,0:T(8,128)(2,1)} %fusion.1) | copy-start | bytes 5898244
  196.3 27.2 %copy-start.3 = (f32[64,768]{1,0:T(8,128)S(1)}, f32[64,768]{1,0:T(8,128)}, u32[]{:S(2)}) copy-start(f32[64,768]{1,0:T(8,128)} %reduce-scatter.7.cloned.1.call-done) | copy-start | bytes 589828
  199.5 76.3 %reduce-scatter.11.cloned.1.call-start = ((), (), s32[]{:S(2)}) async-start(), calls=%async_computation.9 | async-start | bytes 1310720 | tf_op jit(solution)/shard_map/reduce_scatter | solution.py:86
  224.6 21.2 %copy-start.9 = (f32[256,1024]{1,0:T(8,128)S(1)}, f32[256,1024]{1,0:T(8,128)}, u32[]{:S(2)}) copy-start(f32[256,1024]{1,0:T(8,128)} %copy-done.8) | copy-start | bytes 3145732
Sparse Core Ops, SparseCore 0:
  9.5 51.8 all-gather.2
  63.4 48.8 all-gather.4
  115.7 22.9 reduce-scatter.4
  147.0 23.8 reduce-scatter.6
  199.6 23.8 reduce-scatter.8
  250.7 25.0 reduce-scatter.10
where the time goes:
time: 298 us; the launch traced here: 297 us
  waiting for transfers between devices  185 us (62%)
  blocking collectives  63.8 us (21%)
  matrix products  18.7 us (6%)
  between operations  14.3 us (5%)
  other arithmetic  13.1 us (4%)
    all_gather x1, waiting for transfers between devices, local(): w_down = lax.all_gather(down_weight, 'dp', axis=1, tiled=True)  48.5 us
    all_gather x1, waiting for transfers between devices, local(): w_up = lax.all_gather(up_weight, 'dp', axis=0, tiled=True)  44.1 us
    reduce_scatter x1, waiting for transfers between devices, local(): lax.psum_scatter(back_part, 'txt', scatter_dimension=0, tiled=True)  23.9 us
    reduce_scatter x1, waiting for transfers between devices, local(): lax.psum_scatter(normed_part, 'txt', scatter_dimension=1, tiled=True)  23.6 us
    reduce_scatter x1, waiting for transfers between devices, local(): mixed = lax.psum_scatter(mixed_part, 'txt', scatter_dimension=1, tiled=True)  22.2 us
    reduce_scatter x1, waiting for transfers between devices, local(): lax.psum_scatter(emb_part, 'txt', scatter_dimension=0, tiled=True)  21.7 us
    all_gather x1, blocking collectives, local(): gathered = lax.all_gather(resid, 'txt', axis=1, tiled=True)  8.89 us
    all_gather x1, blocking collectives, local(): lax.all_gather(output_gradient.astype(jnp.bfloat16), 'txt', axis=1, tiled...  6.85 us
  transfers between devices with their start and end apart: 6, of which 6 were waited for; matrix products, arithmetic and copies ran while one was open for 2% of the time, Pallas kernels for 0%

commit v1 on v0

--- a/solution.py
+++ b/solution.py
@@ -1,9 +1,28 @@
+import functools
 import jax
 import jax.numpy as jnp
 from jax import lax
 from jax.sharding import PartitionSpec as P
 
 MODEL_WIDTH = 1024
+
+
+def draw_knots(message, dev_axis):
+    nodes = lax.axis_size(dev_axis)
+    s_next = sorted(((m, (m + 1) % nodes) for m in range(nodes)))
+    everything = message
+    copies = [everything]
+    ix = 1
+    while ix < nodes:
+        everything = lax.ppermute(everything, dev_axis, s_next)
+        copies.insert(0, everything)
+        ix = ix + 1
+    parts_out = jnp.concatenate(copies, axis=1)
+    b_now = lax.axis_index(dev_axis)
+    return jnp.roll(parts_out, shift=(b_now + 1) * message.shape[1], axis=1)
+
+
+put_trails = functools.partial(draw_knots, dev_axis="dp")
 
 
 def local(
@@ -31,7 +50,7 @@
     centered_input = (input_rows - input_mean) * input_inverse_deviation
     normed_input = (centered_input * prenorm_gain + prenorm_bias).astype(jnp.bfloat16)
     w_up = lax.all_gather(up_weight, "dp", axis=0, tiled=True)
-    w_down = lax.all_gather(down_weight, "dp", axis=1, tiled=True)
+    w_down = put_trails(down_weight)
     pre_act = jnp.dot(normed_input, w_up, preferred_element_type=jnp.float32) + up_bias
     gate_sig = jax.nn.sigmoid(1.702 * pre_act)
     hidden = (pre_act * gate_sig).astype(jnp.bfloat16)

time: 298 us -> 295 us (0.990)
  waiting for transfers between devices: 185 us -> 169 us
  local copies, waits for them, and re-layouts: 1.7 us -> 13.9 us
    ppermute x0 -> x7, waiting for transfers between devices: none -> 77.1 us  [draw_knots(): everything = lax.ppermute(everything, dev_axis, s_next)]
    all_gather x1 -> x0, waiting for transfers between devices: 48.5 us -> none  [local(): w_down = lax.all_gather(down_weight, 'dp', axis=1, tiled=True)]
    all_gather x1, waiting for transfers between devices: 44.1 us -> 0.01 us  [local(): w_up = lax.all_gather(up_weight, 'dp', axis=0, tiled=True)]
    unnamed x20 -> x43, local copies, waits for them, and re-layouts: 0.05 us -> 12.4 us
    ppermute x0 -> x7, starting transfers between devices: none -> 2.98 us  [draw_knots(): everything = lax.ppermute(everything, dev_axis, s_next)]
  transfers between devices with their start and end apart: 6 -> 12, of which waited for: 6 -> 11; matrix products, arithmetic and copies ran while one was open for 2% -> 5% of each run, Pallas kernels for 0% -> 0%
where the time goes in v1:
time: 295 us; the launch traced here: 294 us
  waiting for transfers between devices  169 us (57%)
  blocking collectives  62.3 us (21%)
  matrix products  18.9 us (6%)
  between operations  14 us (5%)
  local copies, waits for them, and re-layouts  13.9 us (5%)
  other arithmetic  13 us (4%)
  starting transfers between devices  3.15 us (1%)
    ppermute x7, waiting for transfers between devices, draw_knots(): everything = lax.ppermute(everything, dev_axis, s_next)  77.1 us
    reduce_scatter x1, waiting for transfers between devices, local(): lax.psum_scatter(normed_part, 'txt', scatter_dimension=1, tiled=True)  24.2 us
    reduce_scatter x1, waiting for transfers between devices, local(): lax.psum_scatter(back_part, 'txt', scatter_dimension=0, tiled=True)  23.9 us
    reduce_scatter x1, waiting for transfers between devices, local(): mixed = lax.psum_scatter(mixed_part, 'txt', scatter_dimension=1, tiled=True)  21.9 us
    reduce_scatter x1, waiting for transfers between devices, local(): lax.psum_scatter(emb_part, 'txt', scatter_dimension=0, tiled=True)  21.7 us
    unnamed x43, local copies, waits for them, and re-layouts  12.4 us
    all_gather x1, blocking collectives, local(): gathered = lax.all_gather(resid, 'txt', axis=1, tiled=True)  7.42 us
    all_gather x1, blocking collectives, local(): lax.all_gather(output_gradient.astype(jnp.bfloat16), 'txt', axis=1, tiled...  6.85 us
  transfers between devices with their start and end apart: 12, of which 11 were waited for; matrix products, arithmetic and copies ran while one was open for 5% of the time, Pallas kernels for 0%

profile of v1, /device:TPU:0, one launch (start us, length us, event | category | flops | bytes accessed | tf_op | source)
XLA Modules:
  0.0 294.3 jit_solution(16642486355228864485)
XLA Ops:
  9.6 9.5 %collective-permute-done = bf16[1024,128]{1,0:T(8,128)(2,1)S(1)} collective-permute-done((bf16[1024,128]{1,0:T(8,128)(2,1)}, bf16[1024,128]{1,0:T(8,128)(2,1)S(1)}, u32[]{:S(2)}, u32[]{:S(2)}) %collective-permute-start) | collective-permute-done | bytes 262176 | tf_op jit(solution)/shard_map/ppermute | solution.py:17
  19.1 15.3 %collective-permute-done.1 = bf16[1024,128]{1,0:T(8,128)(2,1)S(1)} collective-permute-done((bf16[1024,128]{1,0:T(8,128)(2,1)S(1)}, bf16[1024,128]{1,0:T(8,128)(2,1)S(1)}, u32[]{:S(2)}, u32[]{:S(2)}) %collective-permute-start.1) | collective-permute-done | bytes 262176 | tf_op jit(solution)/shard_map/ppermute | solution.py:17
  34.4 9.1 %collective-permute-done.2 = bf16[1024,128]{1,0:T(8,128)(2,1)S(1)} collective-permute-done((bf16[1024,128]{1,0:T(8,128)(2,1)S(1)}, bf16[1024,128]{1,0:T(8,128)(2,1)S(1)}, u32[]{:S(2)}, u32[]{:S(2)}) %collective-permute-start.2) | collective-permute-done | bytes 262176 | tf_op jit(solution)/shard_map/ppermute | solution.py:17
  43.5 16.1 %collective-permute-done.3 = bf16[1024,128]{1,0:T(8,128)(2,1)S(1)} collective-permute-done((bf16[1024,128]{1,0:T(8,128)(2,1)S(1)}, bf16[1024,128]{1,0:T(8,128)(2,1)S(1)}, u32[]{:S(2)}, u32[]{:S(2)}) %collective-permute-start.3) | collective-permute-done | bytes 262176 | tf_op jit(solution)/shard_map/ppermute | solution.py:17
  59.6 15.9 %collective-permute-done.4 = bf16[1024,128]{1,0:T(8,128)(2,1)S(1)} collective-permute-done((bf16[1024,128]{1,0:T(8,128)(2,1)S(1)}, bf16[1024,128]{1,0:T(8,128)(2,1)S(1)}, u32[]{:S(2)}, u32[]{:S(2)}) %collective-permute-start.4) | collective-permute-done | bytes 262176 | tf_op jit(solution)/shard_map/ppermute | solution.py:17
  75.5 7.4 %all_gather.15 = bf16[256,1024]{1,0:T(8,128)(2,1)S(1)} all-gather(bf16[256,256]{1,0:T(8,128)(2,1)} %param.13), channel_id=1, replica_groups=mesh['dp'=8,'txt'=4] {'txt'}, dimensions={1}, use_global_device_ids=true | all-gather | bytes 655360 | tf_op jit(solution)/shard_map/all_gather | solution.py:45
  84.9 9.6 %collective-permute-done.6 = bf16[1024,128]{1,0:T(8,128)(2,1)S(1)} collective-permute-done((bf16[1024,128]{1,0:T(8,128)(2,1)S(1)}, bf16[1024,128]{1,0:T(8,128)(2,1)S(1)}, u32[]{:S(2)}, u32[]{:S(2)}) %collective-permute-start.6) | collective-permute-done | bytes 262176 | tf_op jit(solution)/shard_map/ppermute | solution.py:17
  109.9 3.5 %fusion.4 = f32[256,1024]{1,0:T(8,128)} fusion(bf16[1024,2048]{1,0:T(8,128)(2,1)} %constant_dynamic-update-slice_fusion, s32[]{:T(128)S(6)} %select_n.19, f32[256,1024]{1,0:T(8,128)S(1)} %convolution_add_fusion), kind=kOutput, calls=%fused_computation.7 | convolution fusion | flops 538443776 | bytes 4194308 | tf_op jit(solution)/shard_map/dot_general | solution.py:57
  114.3 21.9 %reduce-scatter.5.cloned.1.call-done = f32[256,256]{1,0:T(8,128)} async-done(((f32[256,1024]{1,0:T(8,128)}), f32[256,256]{1,0:T(8,128)}) %reduce-scatter.5.cloned.1.call-update) | async-done | bytes 262160 | tf_op jit(solution)/shard_map/reduce_scatter | solution.py:58
  137.2 5.8 %all-reduce.2 = (f32[256]{0:T(256)S(1)}, f32[256]{0:T(256)S(1)}) all-reduce(f32[256]{0:T(256)S(1)} %get-tuple-element.12, f32[256]{0:T(256)S(1)} %get-tuple-element.11), channel_id=1, replica_groups=mesh['dp'=8,'txt'=4] {'txt'}, use_global_device_ids=true, to_apply=%region_6.7 | all-reduce | flops 512 | bytes 4096 | tf_op jit(solution)/shard_map/psum | solution.py:61
  146.6 21.7 %reduce-scatter.7.cloned.1.call-done = f32[64,768]{1,0:T(8,128)} async-done(((f32[256,768]{1,0:T(8,128)}), f32[64,768]{1,0:T(8,128)}) %reduce-scatter.7.cloned.1.call-update) | async-done | bytes 196624 | tf_op jit(solution)/shard_map/reduce_scatter | solution.py:68
  170.4 6.1 %all_gather.17 = bf16[256,768]{1,0:T(8,128)(2,1)S(1)} all-gather(bf16[64,768]{1,0:T(8,128)(2,1)S(1)} %fusion.48), channel_id=1, replica_groups=mesh['dp'=8,'txt'=4] {'txt'}, dimensions={0}, use_global_device_ids=true | all-gather | bytes 491520 | tf_op jit(solution)/shard_map/all_gather | solution.py:71
  176.6 3.4 %fusion.54 = (f32[256]{0:T(256)S(1)}, f32[256,1280]{1,0:T(8,128)}) fusion(bf16[256,768]{1,0:T(8,128)(2,1)S(1)} %all_gather.17, bf16[1280,768]{1,0:T(8,128)(2,1)} %fusion.1), kind=kOutput, calls=%fused_computation.102 | convolution fusion | flops 503971584 | bytes 3671040 | tf_op jit(solution)/shard_map/ie,je->ij/dot_general | solution.py:76
  180.0 6.4 %pmax.7 = f32[256]{0:T(256)S(1)} all-reduce(f32[256]{0:T(256)S(1)} %get-tuple-element.28), channel_id=1, replica_groups=mesh['dp'=8,'txt'=4] {'txt'}, use_global_device_ids=true, to_apply=%region_11.12 | all-reduce | flops 256 | bytes 2048 | tf_op jit(solution)/shard_map/pmax | solution.py:80
  188.1 5.7 %psum.58 = f32[256]{0:T(256)S(1)} all-reduce(f32[256]{0:T(256)S(1)} %fusion.12), channel_id=1, replica_groups=mesh['dp'=8,'txt'=4] {'txt'}, use_global_device_ids=true, to_apply=%region_13.14 | all-reduce | flops 256 | bytes 2048 | tf_op jit(solution)/shard_map/psum | solution.py:82
  193.7 3.2 %fusion.23 = f32[256,768]{1,0:T(8,128)} fusion(bf16[1280,768]{1,0:T(8,128)(2,1)S(1)} %copy-done.2, f32[256,1280]{1,0:T(8,128)} %get-tuple-element.29, s32[256]{0:T(256)S(1)} %broadcast_subtract_fusion, f32[256]{0:T(256)S(1)} %psum.58, f32[256]{0:T(256)S(1)} %pmax.7), kind=kOutput, calls=%fused_computation.31 | convolution fusion | flops 505610240 | bytes 4066304 | tf_op jit(solution)/shard_map/dot_general | solution.py:88
  197.0 23.9 %reduce-scatter.9.cloned.1.call-done = f32[64,768]{1,0:T(8,128)} async-done(((f32[256,768]{1,0:T(8,128)}), f32[64,768]{1,0:T(8,128)}) %reduce-scatter.9.cloned.1.call-update) | async-done | bytes 196624 | tf_op jit(solution)/shard_map/reduce_scatter | solution.py:89
  223.1 6.1 %all_gather.18 = bf16[256,768]{1,0:T(8,128)(2,1)S(1)} all-gather(bf16[64,768]{1,0:T(8,128)(2,1)S(1)} %divide_convert_fusion), channel_id=1, replica_groups=mesh['dp'=8,'txt'=4] {'txt'}, dimensions={0}, use_global_device_ids=true | all-gather | bytes 491520 | tf_op jit(solution)/shard_map/all_gather | solution.py:92
  229.7 6.5 %all-reduce.1 = (f32[256]{0:T(256)S(1)}, f32[256]{0:T(256)S(1)}) all-reduce(f32[256]{0:T(256)S(1)} %get-tuple-element.10, f32[256]{0:T(256)S(1)} %get-tuple-element.9), channel_id=1, replica_groups=mesh['dp'=8,'txt'=4] {'txt'}, use_global_device_ids=true, to_apply=%region_19.20 | all-reduce | flops 512 | bytes 4096 | tf_op jit(solution)/shard_map/psum | solution.py:95
  236.3 6.9 %all_gather.19 = bf16[256,1024]{1,0:T(8,128)(2,1)S(1)} all-gather(bf16[256,256]{1,0:T(8,128)(2,1)S(1)} %get-tuple-element.21), channel_id=1, replica_groups=mesh['dp'=8,'txt'=4] {'txt'}, dimensions={1}, use_global_device_ids=true | all-gather | bytes 655360 | tf_op jit(solution)/shard_map/all_gather | solution.py:99
  243.2 4.7 %fusion.14 = f32[256,1024]{1,0:T(8,128)} fusion(bf16[1024,1024]{1,0:T(8,128)(2,1)} %all-gather.2.cloned.1.call-done, bf16[256,1024]{1,0:T(8,128)(2,1)S(1)} %all_gather.19, bf16[1024,2048]{1,0:T(8,128)(2,1)} %constant_dynamic-update-slice_fusion, s32[]{:T(128)S(6)} %select_n.19, f32[256,1024]{1,0:T(8,128)S(1)} %copy-done.13), kind=kOutput, calls=%fused_computation.20 | convolution fusion | flops 1076363264 | bytes 6815748 | tf_op jit(solution)/shard_map/if,df->id/dot_general | solution.py:104
  248.9 24.2 %reduce-scatter.11.cloned.1.call-done = f32[256,256]{1,0:T(8,128)} async-done(((f32[256,1024]{1,0:T(8,128)}), f32[256,256]{1,0:T(8,128)}) %reduce-scatter.11.cloned.1.call-update) | async-done | bytes 262160 | tf_op jit(solution)/shard_map/reduce_scatter | solution.py:105
  274.3 5.8 %all-reduce = (f32[256]{0:T(256)S(1)}, f32[256]{0:T(256)S(1)}) all-reduce(f32[256]{0:T(256)S(1)} %get-tuple-element.8, f32[256]{0:T(256)S(1)} %get-tuple-element.7), channel_id=1, replica_groups=mesh['dp'=8,'txt'=4] {'txt'}, use_global_device_ids=true, to_apply=%region_24.25 | all-reduce | flops 512 | bytes 4096 | tf_op jit(solution)/shard_map/psum | solution.py:112
  281.3 5.7 %psum.63 = f32[256]{0:T(256)S(1)} all-reduce(f32[256]{0:T(256)S(1)} %get-tuple-element.19), channel_id=1, replica_groups=mesh['dp'=8,'txt'=4] {'txt'}, use_global_device_ids=true, to_apply=%region_26.27 | all-reduce | flops 256 | bytes 2048 | tf_op jit(solution)/shard_map/psum | solution.py:125
  (91 shorter events, 35.9 us)
Async XLA Ops:
  6.5 136.5 %copy-start = (bf16[256,768]{1,0:T(8,128)(2,1)S(1)}, bf16[256,768]{1,0:T(8,128)(2,1)}, u32[]{:S(2)}) copy-start(bf16[256,768]{1,0:T(8,128)(2,1)} %param.22) | copy-start | bytes 1179652
  6.5 93.2 %copy-start.5 = (bf16[1024,128]{1,0:T(8,128)(2,1)S(1)}, bf16[1024,128]{1,0:T(8,128)(2,1)}, u32[]{:S(2)}) copy-start(bf16[1024,128]{1,0:T(8,128)(2,1)} %param.18) | copy-start | bytes 786436
  6.5 100.0 %all-gather.2.cloned.1.call-start = ((), (), s32[]{:S(2)}) async-start(), calls=%async_computation.4 | async-start | bytes 2359296 | tf_op jit(solution)/shard_map/all_gather | solution.py:52
  6.5 12.5 %collective-permute-start = (bf16[1024,128]{1,0:T(8,128)(2,1)}, bf16[1024,128]{1,0:T(8,128)(2,1)S(1)}, u32[]{:S(2)}, u32[]{:S(2)}) collective-permute-start(bf16[1024,128]{1,0:T(8,128)(2,1)} %param.18), channel_id=1, source_target_pairs={{0,4},{4,8},{8,12},{12,16},{16,20},{20,24},{24,28},{28,0},{1,5},{5... | collective-permute-start | bytes 786440 | tf_op jit(solution)/shard_map/ppermute | solution.py:17
  9.5 126.6 %reduce-scatter.5.cloned.1.call-start = ((), (), s32[]{:S(2)}) async-start(), calls=%async_computation.5 | async-start | bytes 1310720 | tf_op jit(solution)/shard_map/reduce_scatter | solution.py:58
  19.1 15.3 %collective-permute-start.1 = (bf16[1024,128]{1,0:T(8,128)(2,1)S(1)}, bf16[1024,128]{1,0:T(8,128)(2,1)S(1)}, u32[]{:S(2)}, u32[]{:S(2)}) collective-permute-start(bf16[1024,128]{1,0:T(8,128)(2,1)S(1)} %collective-permute-done), channel_id=1, source_target_pairs={{0,4},{4,8},{8,12},{12,16},{16,20},{20,24},{24,28},{28,0},{1,5},{5... | collective-permute-start | bytes 786440 | tf_op jit(solution)/shard_map/ppermute | solution.py:17
  34.4 9.1 %collective-permute-start.2 = (bf16[1024,128]{1,0:T(8,128)(2,1)S(1)}, bf16[1024,128]{1,0:T(8,128)(2,1)S(1)}, u32[]{:S(2)}, u32[]{:S(2)}) collective-permute-start(bf16[1024,128]{1,0:T(8,128)(2,1)S(1)} %collective-permute-done.1), channel_id=1, source_target_pairs={{0,4},{4,8},{8,12},{12,16},{16,20},{20,24},{24,28},{28,0},{1,5},{5... | collective-permute-start | bytes 786440 | tf_op jit(solution)/shard_map/ppermute | solution.py:17
  43.5 16.1 %collective-permute-start.3 = (bf16[1024,128]{1,0:T(8,128)(2,1)S(1)}, bf16[1024,128]{1,0:T(8,128)(2,1)S(1)}, u32[]{:S(2)}, u32[]{:S(2)}) collective-permute-start(bf16[1024,128]{1,0:T(8,128)(2,1)S(1)} %collective-permute-done.2), channel_id=1, source_target_pairs={{0,4},{4,8},{8,12},{12,16},{16,20},{20,24},{24,28},{28,0},{1,5},{5... | collective-permute-start | bytes 786440 | tf_op jit(solution)/shard_map/ppermute | solution.py:17
  59.6 15.9 %collective-permute-start.4 = (bf16[1024,128]{1,0:T(8,128)(2,1)S(1)}, bf16[1024,128]{1,0:T(8,128)(2,1)S(1)}, u32[]{:S(2)}, u32[]{:S(2)}) collective-permute-start(bf16[1024,128]{1,0:T(8,128)(2,1)S(1)} %collective-permute-done.3), channel_id=1, source_target_pairs={{0,4},{4,8},{8,12},{12,16},{16,20},{20,24},{24,28},{28,0},{1,5},{5... | collective-permute-start | bytes 786440 | tf_op jit(solution)/shard_map/ppermute | solution.py:17
  75.5 9.1 %collective-permute-start.5 = (bf16[1024,128]{1,0:T(8,128)(2,1)S(1)}, bf16[1024,128]{1,0:T(8,128)(2,1)S(1)}, u32[]{:S(2)}, u32[]{:S(2)}) collective-permute-start(bf16[1024,128]{1,0:T(8,128)(2,1)S(1)} %collective-permute-done.4), channel_id=1, source_target_pairs={{0,4},{4,8},{8,12},{12,16},{16,20},{20,24},{24,28},{28,0},{1,5},{5... | collective-permute-start | bytes 786440 | tf_op jit(solution)/shard_map/ppermute | solution.py:17
  84.6 9.9 %collective-permute-start.6 = (bf16[1024,128]{1,0:T(8,128)(2,1)S(1)}, bf16[1024,128]{1,0:T(8,128)(2,1)S(1)}, u32[]{:S(2)}, u32[]{:S(2)}) collective-permute-start(bf16[1024,128]{1,0:T(8,128)(2,1)S(1)} %collective-permute-done.5), channel_id=1, source_target_pairs={{0,4},{4,8},{8,12},{12,16},{16,20},{20,24},{24,28},{28,0},{1,5},{5... | collective-permute-start | bytes 786440 | tf_op jit(solution)/shard_map/ppermute | solution.py:17
  84.8 21.7 %copy-start.9 = (f32[1024]{0:T(1024)S(1)}, f32[1024]{0:T(1024)}, u32[]{:S(2)}) copy-start(f32[1024]{0:T(1024)} %param.14) | copy-start | bytes 12292
  84.9 21.7 %copy-start.10 = (f32[1024]{0:T(1024)S(1)}, f32[1024]{0:T(1024)}, u32[]{:S(2)}) copy-start(f32[1024]{0:T(1024)} %param.17) | copy-start | bytes 12292
  109.9 26.3 %copy-start.4 = (bf16[256,256]{1,0:T(8,128)(2,1)S(1)}, bf16[256,256]{1,0:T(8,128)(2,1)}, u32[]{:S(2)}) copy-start(bf16[256,256]{1,0:T(8,128)(2,1)} %param.13) | copy-start | bytes 393220
  109.9 33.1 %copy-start.6 = (f32[256]{0:T(256)S(1)}, f32[256]{0:T(256)}, u32[]{:S(2)}) copy-start(f32[256]{0:T(256)} %param.20) | copy-start | bytes 3076
  109.9 33.1 %copy-start.8 = (f32[256]{0:T(256)S(1)}, f32[256]{0:T(256)}, u32[]{:S(2)}) copy-start(f32[256]{0:T(256)} %param.21) | copy-start | bytes 3076
  109.9 34.5 %copy-start.7 = (s32[256]{0:T(256)S(1)}, s32[256]{0:T(256)}, u32[]{:S(2)}) copy-start(s32[256]{0:T(256)} %param.24) | copy-start | bytes 3076
  109.9 34.5 %copy-start.1 = (bf16[1280,768]{1,0:T(8,128)(2,1)S(1)}, bf16[1280,768]{1,0:T(8,128)(2,1)}, u32[]{:S(2)}) copy-start(bf16[1280,768]{1,0:T(8,128)(2,1)} %param.23) | copy-start | bytes 5898244
  113.5 54.9 %reduce-scatter.7.cloned.1.call-start = ((), (), s32[]{:S(2)}) async-start(), calls=%async_computation.6 | async-start | bytes 983040 | tf_op jit(solution)/shard_map/reduce_scatter | solution.py:68
  144.4 76.6 %reduce-scatter.9.cloned.1.call-start = ((), (), s32[]{:S(2)}) async-start(), calls=%async_computation.7 | async-start | bytes 983040 | tf_op jit(solution)/shard_map/reduce_scatter | solution.py:89
  146.6 47.1 %copy-start.2 = (bf16[1280,768]{1,0:T(8,128)(2,1)S(1)}, bf16[1280,768]{1,0:T(8,128)(2,1)}, u32[]{:S(2)}) copy-start(bf16[1280,768]{1,0:T(8,128)(2,1)} %fusion.1) | copy-start | bytes 5898244
  193.7 27.2 %copy-start.3 = (f32[64,768]{1,0:T(8,128)S(1)}, f32[64,768]{1,0:T(8,128)}, u32[]{:S(2)}) copy-start(f32[64,768]{1,0:T(8,128)} %reduce-scatter.7.cloned.1.call-done) | copy-start | bytes 589828
  196.9 46.3 %copy-start.13 = (f32[256,1024]{1,0:T(8,128)S(1)}, f32[256,1024]{1,0:T(8,128)}, u32[]{:S(2)}) copy-start(f32[256,1024]{1,0:T(8,128)} %copy-done.12) | copy-start | bytes 3145732
  196.9 76.2 %reduce-scatter.11.cloned.1.call-start = ((), (), s32[]{:S(2)}) async-start(), calls=%async_computation.8 | async-start | bytes 1310720 | tf_op jit(solution)/shard_map/reduce_scatter | solution.py:105
  (2 other events, 22.7 us)
Sparse Core Ops, SparseCore 0:
  9.7 61.9 all-gather.1
  113.6 22.5 reduce-scatter.4
  144.5 23.8 reduce-scatter.6
  197.0 23.8 reduce-scatter.8
  248.1 25.0 reduce-scatter.10
